TPU v7x, 512 devices: a 4x2x32 block of a 4x8x32 slice. The times are simulated.
512 devices in a mesh: groups: 2 (over y), expert: 32 (over z), tensor: 8 (over x, core).
Axes of the slice: x: 4, y: 2, z: 32, core: 2. Of those that a mesh axis runs over, the one named last changes fastest.
The devices are a block of a 4x8x32 slice.
Arguments:
- tokens: bfloat16 [8192, 7168], P(('groups', 'expert'), 'tensor'), parts along dimension 0, may hold values from -6 to 6
- choices: int32 [8192, 4], P(('groups', 'expert')), parts along dimension 0, may hold values from 0 to 15, all different within a row; in each aligned block of 128 rows (0 to 127, 128 to 255, ...) at most 48 rows name the same one
- affinity: float32 [8192, 4], P(('groups', 'expert')), parts along dimension 0, may hold values from -6 to 6
- expert_gate: bfloat16 [7168, 16384], P('tensor', 'expert'), may hold values from -0.0625 to 0.0625
- expert_up: bfloat16 [7168, 16384], P('tensor', 'expert'), may hold values from -0.0625 to 0.0625
- expert_down: bfloat16 [16384, 7168], P('expert', 'tensor'), may hold values from -0.1875 to 0.1875
- shared_in: bfloat16 [2, 1024, 7168], P(None, 'expert', 'tensor'), may hold values from -0.0625 to 0.0625
- shared_down: bfloat16 [1024, 7168], P('expert', 'tensor'), may hold values from -0.1875 to 0.1875
Outputs:
- mixed: bfloat16 [8192, 7168], P(('groups', 'expert'), 'tensor'), parts along dimension 0
There are 2 independent parts, one for each index of `groups`. A program takes and returns all parts, laid end to end along the dimension named above; an argument that names none is the same for every part. Nothing has to cross between parts.
Inputs may be any that keep to these rules, and one draw needn't show every extreme that they name: `choices`: within the rows of one index of expert (128 tokens) every expert is named at most 48 times, a bound that some block reaches; a token names 4 different experts.
All inputs are finite; a program needn't handle non-finite values.
Results may differ from a plain program's by a relative error of at most 0.02.
Values may be sent and summed in bfloat16 or wider, within the bound.
No kernel may reach another device: no remote copies, remote signals or barrier semaphores. Data moves between devices by JAX's collectives and lax.ppermute only.
A program may use at most 64 MiB of HBM per device.

v0:
```python
import jax
import jax.numpy as jnp
from jax import lax
from jax.sharding import PartitionSpec as P

FFE = 1024
EXPERTS = 16
TOP = 4
CAP = 48


def local(tokens, choices, affinity, expert_gate, expert_up, expert_down, shared_in, shared_down):
    tok_rows = tokens.shape[0]
    width_slice = tokens.shape[1]
    expert_count = lax.axis_size("expert")
    column_count = expert_gate.shape[1]
    piece_width = min(FFE, column_count)
    local_count = column_count // piece_width
    split_count = FFE // piece_width
    sigmoids = jax.nn.sigmoid(affinity)
    mix = 2.5 * sigmoids / jnp.sum(sigmoids, axis=1, keepdims=True)
    flat_ids = choices.reshape(-1)
    onehot = (flat_ids[:, None] == jnp.arange(EXPERTS, dtype=jnp.int32)[None, :]).astype(jnp.int32)
    earlier = jnp.cumsum(onehot, axis=0) - onehot
    position = jnp.sum(earlier * onehot, axis=1)
    slot_ids = flat_ids * CAP + position
    row_owner = jnp.arange(tok_rows * TOP, dtype=jnp.int32) // TOP
    source_row = jnp.zeros((EXPERTS * CAP,), jnp.int32).at[slot_ids].set(row_owner)
    filled = jnp.zeros((EXPERTS * CAP,), jnp.int32).at[slot_ids].set(1)
    packed = jnp.where(filled[:, None] > 0, tokens[source_row], jnp.zeros((), jnp.bfloat16))
    outbound = jnp.broadcast_to(
        packed.reshape(EXPERTS, 1, CAP, width_slice), (EXPERTS, split_count, CAP, width_slice)
    )
    outbound = outbound.reshape(expert_count, local_count, CAP, width_slice)
    gate_cols = expert_gate.reshape(width_slice, local_count, piece_width)
    up_cols = expert_up.reshape(width_slice, local_count, piece_width)
    down_rows = expert_down.reshape(local_count, piece_width, width_slice)
    received = lax.all_to_all(outbound, "expert", split_axis=0, concat_axis=0, tiled=True)
    gate_part = jnp.einsum(
        "nlcd,dlp->nlcp", received, gate_cols, preferred_element_type=jnp.float32
    )
    up_part = jnp.einsum("nlcd,dlp->nlcp", received, up_cols, preferred_element_type=jnp.float32)
    gate_sum = lax.psum(gate_part.astype(jnp.bfloat16), "tensor").astype(jnp.float32)
    up_sum = lax.psum(up_part.astype(jnp.bfloat16), "tensor").astype(jnp.float32)
    hidden = (jax.nn.silu(gate_sum) * up_sum).astype(jnp.bfloat16)
    produced = jnp.einsum("nlcp,lpd->nlcd", hidden, down_rows, preferred_element_type=jnp.float32)
    returned = lax.all_to_all(
        produced.astype(jnp.bfloat16), "expert", split_axis=0, concat_axis=0, tiled=True
    )
    summed = jnp.sum(
        returned.astype(jnp.float32).reshape(EXPERTS, split_count, CAP, width_slice), axis=1
    )
    picked = summed.reshape(EXPERTS * CAP, width_slice)[slot_ids].reshape(
        tok_rows, TOP, width_slice
    )
    routed = jnp.sum(mix[:, :, None] * picked, axis=1)
    terms = jnp.einsum(
        "td,gnd->gtn",
        tokens,
        lax.all_gather(shared_in, "expert", axis=1, tiled=True),
        preferred_element_type=jnp.float32,
    )
    sums = lax.psum(terms.astype(jnp.bfloat16), "tensor").astype(jnp.float32)
    shared_hidden = (jax.nn.silu(sums[0]) * sums[1]).astype(jnp.bfloat16)
    shared_out = jnp.dot(
        shared_hidden,
        lax.all_gather(shared_down, "expert", axis=0, tiled=True),
        preferred_element_type=jnp.float32,
    )
    return (routed + shared_out).astype(jnp.bfloat16)


def solution(mesh):
    placed = (
        P(("groups", "expert"), "tensor"),
        P(("groups", "expert"), None),
        P(("groups", "expert"), None),
        P("tensor", "expert"),
        P("tensor", "expert"),
        P("expert", "tensor"),
        P(None, "expert", "tensor"),
        P("expert", "tensor"),
    )
    return jax.shard_map(
        local,
        mesh=mesh,
        in_specs=placed,
        out_specs=P(("groups", "expert"), "tensor"),
        check_vma=False,
    )
```

profile of v0, /device:TPU:96, one launch (start us, length us, event | category | flops | bytes accessed | tf_op | source)
XLA Modules:
  0.0 806.6 jit_solution(5608995960913174588)
XLA Ops:
  6.5 0.0 copy-start
  6.6 0.0 copy-start.1
  6.6 0.9 copy.17
  7.4 0.1 eq.29
  7.5 0.1 eq.25
  7.6 0.7 broadcast_multiply_fusion
  8.3 1.2 reduce-window.6
  9.5 0.2 slice_reduce_fusion
  9.8 0.1 copy.16
  9.9 0.1 mul.52
  10.0 0.1 fusion.35
  10.1 2.4 scatter_custom_fusion.1
  12.6 2.4 scatter_custom_fusion
  15.1 0.1 broadcast_in_dim.33
  15.1 0.0 copy-done.1
  15.1 2.8 gather_fusion
  18.0 0.2 broadcast_select_fusion
  18.2 1.8 broadcast_in_dim.37
  20.0 44.3 %all-to-all-start = ((bf16[32,1,48,896]{3,2,1,0:T(8,128)(2,1)}), bf16[32,1,48,896]{3,2,1,0:T(8,128)(2,1)}, u32[]{:S(2)}, u32[]{:S(2)}) async-start(bf16[32,1,48,896]{3,2,1,0:T(8,128)(2,1)} %bitcast.93), calls=%async_computation | async-start | bytes 5505024 | tf_op jit(solution)/shard_map/all_to_all | solution.py:38
  64.3 0.0 copy-start.4
  64.3 0.1 all-gather.3.cloned.1.call-start
  64.4 0.7 all-gather.3.cloned.1.call-update
  65.1 0.1 all-reduce.3.cloned.1.call-start
  65.2 305.2 %all-gather.3.cloned.1.call-done = bf16[2,1024,896]{2,1,0:T(8,128)(2,1)} async-done(((bf16[2,32,896]{2,1,0:T(8,128)(2,1)}), bf16[2,1024,896]{2,1,0:T(8,128)(2,1)}) %all-gather.3.cloned.1.call-update) | async-done | bytes 3670032 | tf_op jit(solution)/shard_map/all_gather | solution.py:60
  370.4 4.0 fusion.23
  374.4 0.0 copy-start.5
  374.4 0.0 all-to-all-done
  374.4 0.0 copy-done.4
  374.4 4.8 fusion.17
  379.2 0.0 copy-done.5
  379.2 4.7 fusion.20
  383.9 0.1 all-reduce.3.cloned.1.call-update
  384.0 99.2 %all-reduce.3.cloned.1.call-done = (bf16[32,1,48,512]{3,2,0,1:T(8,128)(2,1)}, bf16[32,1,48,512]{3,2,0,1:T(8,128)(2,1)}, bf16[2,128,1024]{1,2,0:T(8,128)(2,1)}) async-done(((bf16[32,1,48,512]{3,2,0,1:T(8,128)(2,1)}, bf16[32,1,48,512]{3,2,0,1:T(8,128)(2,1)}, bf16[2,128,1024]{1,2,0:T(8,128)(2,1)}), (bf16[32,1,48,512]{3,2,0,1:T(8,128)(2,1)}, bf16[32,1,48,512]{3,2,0,1:T(8,128)(2,1)}, ...) | async-done | bytes 3670032 | tf_op jit(solution)/shard_map/psum | solution.py:44
  483.2 0.0 copy-done
  483.2 5.5 convert_bitcast_fusion
  488.7 0.0 copy-start.3
  488.7 0.0 copy-start.2
  488.7 23.4 %all-to-all-start.1 = ((bf16[32,1,48,896]{3,2,1,0:T(8,128)(2,1)}), bf16[32,1,48,896]{3,2,1,0:T(8,128)(2,1)}, u32[]{:S(2)}, u32[]{:S(2)}) async-start(bf16[32,1,48,896]{3,2,1,0:T(8,128)(2,1)} %convert_bitcast_fusion), calls=%async_computation.1 | async-start | bytes 5505024 | tf_op jit(solution)/shard_map/all_to_all | solution.py:47
  512.1 0.2 all-gather.5.cloned.1.call-start
  512.3 0.5 all-gather.5.cloned.1.call-update
  512.9 0.0 copy-done.3
  512.9 0.1 copy.15
  513.1 0.0 copy-done.2
  513.1 1.0 convert_element_type.87
  514.1 270.0 %all-to-all-done.1 = bf16[32,1,48,896]{3,2,1,0:T(8,128)(2,1)} async-done(((bf16[32,1,48,896]{3,2,1,0:T(8,128)(2,1)}), bf16[32,1,48,896]{3,2,1,0:T(8,128)(2,1)}, u32[]{:S(2)}, u32[]{:S(2)}) %all-to-all-start.1) | async-done | bytes 2752544 | tf_op jit(solution)/shard_map/all_to_all | solution.py:47
  784.1 4.0 convert_reduce_fusion
  788.2 4.4 gather_fusion.1
  792.6 1.8 reshape.107
  794.4 2.7 multiply_reduce_fusion
  797.0 0.0 all-gather.5.cloned.1.call-done
  797.1 3.0 fusion.24
  (12 shorter events, 0.1 us)
Async XLA Ops:
  6.5 476.6 %copy-start = (bf16[512,896]{1,0:T(8,128)(2,1)S(1)}, bf16[512,896]{1,0:T(8,128)(2,1)}, u32[]{:S(2)}) copy-start(bf16[512,896]{1,0:T(8,128)(2,1)} %param.13) | copy-start | bytes 2752516
  6.6 8.6 %copy-start.1 = (bf16[128,896]{1,0:T(8,128)(2,1)S(1)}, bf16[128,896]{1,0:T(8,128)(2,1)}, u32[]{:S(2)}) copy-start(bf16[128,896]{1,0:T(8,128)(2,1)} %param.8) | copy-start | bytes 688132
  20.0 354.4 %all-to-all-start = ((bf16[32,1,48,896]{3,2,1,0:T(8,128)(2,1)}), bf16[32,1,48,896]{3,2,1,0:T(8,128)(2,1)}, u32[]{:S(2)}, u32[]{:S(2)}) async-start(bf16[32,1,48,896]{3,2,1,0:T(8,128)(2,1)} %bitcast.93), calls=%async_computation | async-start | bytes 5505024 | tf_op jit(solution)/shard_map/all_to_all | solution.py:38
  64.3 310.0 %copy-start.4 = (bf16[896,512]{1,0:T(8,128)(2,1)S(1)}, bf16[896,512]{1,0:T(8,128)(2,1)}, u32[]{:S(2)}) copy-start(bf16[896,512]{1,0:T(8,128)(2,1)} %param.12) | copy-start | bytes 2752516
  64.3 306.1 %all-gather.3.cloned.1.call-start = ((), (), s32[]{:S(2)}) async-start(), calls=%async_computation.2 | async-start | bytes 3784704 | tf_op jit(solution)/shard_map/all_gather | solution.py:60
  65.1 418.0 %all-reduce.3.cloned.1.call-start = ((), (), s32[]{:S(2)}) async-start(), calls=%async_computation.4 | async-start | bytes 7340032 | tf_op jit(solution)/shard_map/psum | solution.py:44
  374.4 4.8 copy-start.5
  488.7 24.2 %copy-start.3 = (f32[128,4]{0,1:T(4,128)S(1)}, f32[128,4]{0,1:T(4,128)}, u32[]{:S(2)}) copy-start(f32[128,4]{0,1:T(4,128)} %param.10) | copy-start | bytes 6148
  488.7 24.4 %copy-start.2 = (bf16[2,128,1024]{1,2,0:T(8,128)(2,1)S(1)}, bf16[2,128,1024]{1,2,0:T(8,128)(2,1)}, u32[]{:S(2)}) copy-start(bf16[2,128,1024]{1,2,0:T(8,128)(2,1)} %get-tuple-element.7) | copy-start | bytes 1572868
  488.7 295.4 %all-to-all-start.1 = ((bf16[32,1,48,896]{3,2,1,0:T(8,128)(2,1)}), bf16[32,1,48,896]{3,2,1,0:T(8,128)(2,1)}, u32[]{:S(2)}, u32[]{:S(2)}) async-start(bf16[32,1,48,896]{3,2,1,0:T(8,128)(2,1)} %convert_bitcast_fusion), calls=%async_computation.1 | async-start | bytes 5505024 | tf_op jit(solution)/shard_map/all_to_all | solution.py:47
  512.1 285.0 %all-gather.5.cloned.1.call-start = ((), (), s32[]{:S(2)}) async-start(), calls=%async_computation.3 | async-start | bytes 1892352 | tf_op jit(solution)/shard_map/all_gather | solution.py:67
Sparse Core Ops, SparseCore 0:
  67.3 303.0 all-gather.2
  384.1 99.0 all-reduce.2
  515.0 246.0 all-gather.4
where the time goes:
time: 807 us
  waiting for transfers between devices  676 us (84%)
  starting transfers between devices  68.1 us (8%)
  matrix products  22 us (3%)
  local copies, waits for them, and re-layouts  17.5 us (2%)
  between operations  13.3 us (2%)
  other arithmetic  10 us (1%)
    all_gather x1, waiting for transfers between devices, local(): lax.all_gather(shared_in, 'expert', axis=1, tiled=True)  305 us
    all_to_all x1, waiting for transfers between devices, local(): lax.all_to_all(produced.astype(jnp.bfloat16), 'expert', split_axis=0, con...  270 us
    psum x1, waiting for transfers between devices, local(): lax.psum(up_part.astype(jnp.bfloat16), 'tensor').astype(jnp.float32)  99.2 us
    all_to_all x1, starting transfers between devices, local(): lax.all_to_all(outbound, 'expert', split_axis=0, concat_axis=0, tiled=True)  44.3 us
    all_to_all x1, starting transfers between devices, local(): lax.all_to_all(produced.astype(jnp.bfloat16), 'expert', split_axis=0, con...  23.4 us
  transfers between devices with their start and end apart: 5, of which 3 were waited for; matrix products, arithmetic and copies ran while one was open for 2% of the time, Pallas kernels for 0%

commit v1 on v0

--- a/solution.py
+++ b/solution.py
@@ -41,7 +41,9 @@
     )
     up_part = jnp.einsum("nlcd,dlp->nlcp", received, up_cols, preferred_element_type=jnp.float32)
     gate_sum = lax.psum(gate_part.astype(jnp.bfloat16), "tensor").astype(jnp.float32)
-    up_sum = lax.psum(up_part.astype(jnp.bfloat16), "tensor").astype(jnp.float32)
+    up_sum = jnp.sum(lax.all_gather(up_part.astype(jnp.bfloat16), "tensor"), axis=0).astype(
+        jnp.float32
+    )
     hidden = (jax.nn.silu(gate_sum) * up_sum).astype(jnp.bfloat16)
     produced = jnp.einsum("nlcp,lpd->nlcd", hidden, down_rows, preferred_element_type=jnp.float32)
     returned = lax.all_to_all(

time: 807 us -> 877 us (1.087)
  the two profiles are of different devices: /device:TPU:96 before, /device:TPU:166 now
where the time goes in v1:
time: 877 us; the launch traced here: 876 us
  waiting for transfers between devices  740 us (84%)
  starting transfers between devices  66.9 us (8%)
  matrix products  21.4 us (2%)
  local copies, waits for them, and re-layouts  17.4 us (2%)
  other arithmetic  17.1 us (2%)
  between operations  13.3 us (2%)
    all_to_all x1, waiting for transfers between devices, local(): lax.all_to_all(outbound, 'expert', split_axis=0, concat_axis=0, tiled=True)  270 us
    all_to_all x1, waiting for transfers between devices, local(): lax.all_to_all(produced.astype(jnp.bfloat16), 'expert', split_axis=0, con...  259 us
    psum x1, waiting for transfers between devices, local(): lax.psum(gate_part.astype(jnp.bfloat16), 'tensor').astype(jnp.float32)  93.6 us
    all_gather x1, waiting for transfers between devices, local(): lax.all_gather(up_part.astype(jnp.bfloat16), 'tensor')  72 us
    all_to_all x1, starting transfers between devices, local(): lax.all_to_all(outbound, 'expert', split_axis=0, concat_axis=0, tiled=True)  43.1 us
    all_gather x1, waiting for transfers between devices, local(): lax.all_gather(shared_in, 'expert', axis=1, tiled=True)  28.8 us
    all_to_all x1, starting transfers between devices, local(): lax.all_to_all(produced.astype(jnp.bfloat16), 'expert', split_axis=0, con...  23.3 us
  transfers between devices with their start and end apart: 6, of which 6 were waited for; matrix products, arithmetic and copies ran while one was open for 4% of the time, Pallas kernels for 0%

profile of v1, /device:TPU:166, one launch (start us, length us, event | category | flops | bytes accessed | tf_op | source)
XLA Modules:
  0.0 875.9 jit_solution(13561633368347364298)
XLA Ops:
  6.5 0.0 copy-start
  6.6 0.0 copy-start.1
  6.6 0.9 copy.17
  7.4 0.1 eq.29
  7.5 0.1 eq.25
  7.6 0.7 broadcast_multiply_fusion
  8.3 1.2 reduce-window.6
  9.5 0.2 slice_reduce_fusion
  9.8 0.1 copy.16
  9.9 0.1 mul.52
  10.0 0.1 fusion.35
  10.1 2.4 scatter_custom_fusion.1
  12.6 2.4 scatter_custom_fusion
  15.1 0.1 broadcast_in_dim.33
  15.1 0.0 copy-done.1
  15.1 2.8 gather_fusion
  18.0 0.2 broadcast_select_fusion
  18.2 1.8 broadcast_in_dim.37
  20.0 0.0 copy-start.4
  20.0 43.1 %all-to-all-start = ((bf16[32,1,48,896]{3,2,1,0:T(8,128)(2,1)}), bf16[32,1,48,896]{3,2,1,0:T(8,128)(2,1)}, u32[]{:S(2)}, u32[]{:S(2)}) async-start(bf16[32,1,48,896]{3,2,1,0:T(8,128)(2,1)} %bitcast.105), calls=%async_computation | async-start | bytes 5505024 | tf_op jit(solution)/shard_map/all_to_all | solution.py:38
  63.1 0.1 all-gather.5.cloned.1.call-start
  63.2 0.7 all-gather.5.cloned.1.call-update
  63.9 0.1 all-gather.9.cloned.1.call-start
  64.0 270.1 %all-to-all-done = bf16[32,1,48,896]{3,2,1,0:T(8,128)(2,1)} async-done(((bf16[32,1,48,896]{3,2,1,0:T(8,128)(2,1)}), bf16[32,1,48,896]{3,2,1,0:T(8,128)(2,1)}, u32[]{:S(2)}, u32[]{:S(2)}) %all-to-all-start) | async-done | bytes 2752544 | tf_op jit(solution)/shard_map/all_to_all | solution.py:38
  334.0 0.0 copy-done.4
  334.0 4.7 fusion.17
  338.8 0.0 copy-start.5
  338.8 0.1 all-gather.9.cloned.1.call-update
  338.8 0.2 all-reduce.3.cloned.1.call-start
  339.1 28.8 %all-gather.5.cloned.1.call-done = bf16[2,1024,896]{2,1,0:T(8,128)(2,1)} async-done(((bf16[2,32,896]{2,1,0:T(8,128)(2,1)}), bf16[2,1024,896]{2,1,0:T(8,128)(2,1)}) %all-gather.5.cloned.1.call-update) | async-done | bytes 3670032 | tf_op jit(solution)/shard_map/all_gather | solution.py:62
  367.9 3.9 fusion.23
  371.8 0.0 copy-done.5
  371.8 4.7 fusion.20
  376.5 0.1 all-reduce.3.cloned.1.call-update
  376.6 72.0 %all-gather.9.cloned.1.call-done = bf16[256,1,48,512]{3,2,1,0:T(8,128)(2,1)} async-done(((bf16[32,1,48,512]{3,2,1,0:T(8,128)(2,1)}), bf16[256,1,48,512]{3,2,1,0:T(8,128)(2,1)}) %all-gather.9.cloned.1.call-update) | async-done | bytes 12582928 | tf_op jit(solution)/shard_map/all_gather | solution.py:44
  448.6 7.1 bitcast_reduce_fusion
  455.7 93.6 %all-reduce.3.cloned.1.call-done = (bf16[32,1,48,512]{3,2,0,1:T(8,128)(2,1)}, bf16[2,128,1024]{1,2,0:T(8,128)(2,1)}) async-done(((bf16[32,1,48,512]{3,2,0,1:T(8,128)(2,1)}, bf16[2,128,1024]{1,2,0:T(8,128)(2,1)}), (bf16[32,1,48,512]{3,2,0,1:T(8,128)(2,1)}, bf16[2,128,1024]{1,2,0:T(8,128)(2,1)})) %all-reduce.3.cloned.1.call-update) | async-done | bytes 2097168 | tf_op jit(solution)/shard_map/psum | solution.py:43
  549.3 0.0 copy-done
  549.3 5.0 convert_bitcast_fusion
  554.3 0.0 copy-start.3
  554.3 0.0 copy-start.2
  554.3 23.3 %all-to-all-start.1 = ((bf16[32,1,48,896]{3,2,1,0:T(8,128)(2,1)}), bf16[32,1,48,896]{3,2,1,0:T(8,128)(2,1)}, u32[]{:S(2)}, u32[]{:S(2)}) async-start(bf16[32,1,48,896]{3,2,1,0:T(8,128)(2,1)} %convert_bitcast_fusion), calls=%async_computation.1 | async-start | bytes 5505024 | tf_op jit(solution)/shard_map/all_to_all | solution.py:49
  577.6 0.1 all-gather.7.cloned.1.call-start
  577.7 0.6 all-gather.7.cloned.1.call-update
  578.3 0.0 copy-done.3
  578.3 0.1 copy.15
  578.4 0.0 copy-done.2
  578.5 1.0 convert_element_type.101
  579.5 259.4 %all-to-all-done.1 = bf16[32,1,48,896]{3,2,1,0:T(8,128)(2,1)} async-done(((bf16[32,1,48,896]{3,2,1,0:T(8,128)(2,1)}), bf16[32,1,48,896]{3,2,1,0:T(8,128)(2,1)}, u32[]{:S(2)}, u32[]{:S(2)}) %all-to-all-start.1) | async-done | bytes 2752544 | tf_op jit(solution)/shard_map/all_to_all | solution.py:49
  838.9 4.0 convert_reduce_fusion
  843.0 4.4 gather_fusion.1
  847.4 1.8 reshape.118
  849.2 2.7 multiply_reduce_fusion
  851.8 14.5 %all-gather.7.cloned.1.call-done = bf16[1024,896]{1,0:T(8,128)(2,1)} async-done(((bf16[32,896]{1,0:T(8,128)(2,1)}), bf16[1024,896]{1,0:T(8,128)(2,1)}) %all-gather.7.cloned.1.call-update) | async-done | bytes 1835024 | tf_op jit(solution)/shard_map/all_gather | solution.py:69
  866.3 3.0 fusion.24
  (12 shorter events, 0.1 us)
Async XLA Ops:
  6.5 542.7 %copy-start = (bf16[512,896]{1,0:T(8,128)(2,1)S(1)}, bf16[512,896]{1,0:T(8,128)(2,1)}, u32[]{:S(2)}) copy-start(bf16[512,896]{1,0:T(8,128)(2,1)} %param.13) | copy-start | bytes 2752516
  6.6 8.6 copy-start.1
  20.0 314.1 %copy-start.4 = (bf16[896,512]{1,0:T(8,128)(2,1)S(1)}, bf16[896,512]{1,0:T(8,128)(2,1)}, u32[]{:S(2)}) copy-start(bf16[896,512]{1,0:T(8,128)(2,1)} %param.12) | copy-start | bytes 2752516
  20.0 314.1 %all-to-all-start = ((bf16[32,1,48,896]{3,2,1,0:T(8,128)(2,1)}), bf16[32,1,48,896]{3,2,1,0:T(8,128)(2,1)}, u32[]{:S(2)}, u32[]{:S(2)}) async-start(bf16[32,1,48,896]{3,2,1,0:T(8,128)(2,1)} %bitcast.105), calls=%async_computation | async-start | bytes 5505024 | tf_op jit(solution)/shard_map/all_to_all | solution.py:38
  63.1 304.8 %all-gather.5.cloned.1.call-start = ((), (), s32[]{:S(2)}) async-start(), calls=%async_computation.2 | async-start | bytes 3784704 | tf_op jit(solution)/shard_map/all_gather | solution.py:62
  63.9 384.7 %all-gather.9.cloned.1.call-start = ((), (), s32[]{:S(2)}) async-start(), calls=%async_computation.4 | async-start | bytes 14155776 | tf_op jit(solution)/shard_map/all_gather | solution.py:44
  338.8 33.0 %copy-start.5 = (bf16[896,512]{1,0:T(8,128)(2,1)S(1)}, bf16[896,512]{1,0:T(8,128)(2,1)}, u32[]{:S(2)}) copy-start(bf16[896,512]{1,0:T(8,128)(2,1)} %param.11) | copy-start | bytes 2752516
  338.8 210.4 %all-reduce.3.cloned.1.call-start = ((), (), s32[]{:S(2)}) async-start(), calls=%async_computation.5 | async-start | bytes 4194304 | tf_op jit(solution)/shard_map/psum | solution.py:43
  554.3 24.0 %copy-start.3 = (f32[128,4]{0,1:T(4,128)S(1)}, f32[128,4]{0,1:T(4,128)}, u32[]{:S(2)}) copy-start(f32[128,4]{0,1:T(4,128)} %param.10) | copy-start | bytes 6148
  554.3 24.2 %copy-start.2 = (bf16[2,128,1024]{1,2,0:T(8,128)(2,1)S(1)}, bf16[2,128,1024]{1,2,0:T(8,128)(2,1)}, u32[]{:S(2)}) copy-start(bf16[2,128,1024]{1,2,0:T(8,128)(2,1)} %get-tuple-element.6) | copy-start | bytes 1572868
  554.3 284.6 %all-to-all-start.1 = ((bf16[32,1,48,896]{3,2,1,0:T(8,128)(2,1)}), bf16[32,1,48,896]{3,2,1,0:T(8,128)(2,1)}, u32[]{:S(2)}, u32[]{:S(2)}) async-start(bf16[32,1,48,896]{3,2,1,0:T(8,128)(2,1)} %convert_bitcast_fusion), calls=%async_computation.1 | async-start | bytes 5505024 | tf_op jit(solution)/shard_map/all_to_all | solution.py:49
  577.6 288.7 %all-gather.7.cloned.1.call-start = ((), (), s32[]{:S(2)}) async-start(), calls=%async_computation.3 | async-start | bytes 1892352 | tf_op jit(solution)/shard_map/all_gather | solution.py:69
Sparse Core Ops, SparseCore 0:
  66.0 301.7 all-gather.4
  370.0 78.5 all-gather.8
  451.1 98.1 all-reduce.2
  580.2 286.0 all-gather.6
